TPU v7x, 32 devices: a whole 2x2x4 slice. The times are simulated.
32 devices in a mesh: rows: 8 (over z, y), cols: 4 (over x, core).
Axes of the slice: x: 2, y: 2, z: 4, core: 2. Of those that a mesh axis runs over, the one named last changes fastest.
Arguments:
- adjacency_tiles: bfloat16 [192, 12, 128, 128], P(('rows', 'cols')), may hold values from 2.170139e-08 to 0.25
- col_block: int32 [192, 12], P(('rows', 'cols')), may hold values from 0 to 191, as said below
- label_prior: float32 [24576, 256], P(('rows', 'cols')), may hold values from 0.05 to 20.1
- seed_label: int32 [24576], P(('rows', 'cols')), may hold values from 0 to 255
- seed_mask: int32 [24576], P(('rows', 'cols')), may hold values 0 or 1
Outputs:
- labels: float32 [24576, 256], P(('rows', 'cols'))
Inputs may be any that keep to these rules, and one draw needn't show every extreme that they name: Row block b is held by device b // 6 of rows+cols, whose rows group is b // (6 * 4). col_block[b, 0] = b. For each device, all its tiles that reference blocks of another rows group reference one and the same block of that group, and each device references every rows group.
All inputs are finite; a program needn't handle non-finite values. No bound on the sum of `seed_mask` on one device may be relied on, other than what follows from the above.
Results may differ from a plain program's by a relative error of at most 0.00041.
Values may be sent and summed in bfloat16 or wider, within the bound.
A program may use at most 64 MiB of HBM per device.

v0:
```python
import jax
import jax.numpy as jnp
from jax import lax
from jax.sharding import PartitionSpec as P

HOPS = 4


ALPHA = 0.85
SEED_BOOST = 8.0


def prepare(label_prior, seed_label, seed_mask):
    classes = label_prior.shape[1]
    one_hot = (seed_label[:, None] == jnp.arange(classes, dtype=jnp.int32)[None, :]).astype(
        jnp.float32
    )
    anchor_raw = label_prior + SEED_BOOST * seed_mask[:, None].astype(jnp.float32) * one_hot
    return anchor_raw * (classes / jnp.sum(anchor_raw, axis=1, keepdims=True))


def ask_blocks(owner_group, within, own_group, n_rows):
    group_ids = jnp.arange(n_rows, dtype=jnp.int32)
    matched = owner_group.reshape(-1)[:, None] == group_ids[None, :]
    wanted = jnp.max(jnp.where(matched, within.reshape(-1)[:, None], 0), axis=0)
    wanted = jnp.where(group_ids == own_group, 0, wanted)
    return lax.all_to_all(
        wanted.reshape(n_rows, 1), "rows", split_axis=0, concat_axis=0, tiled=True
    )


def local(adjacency_tiles, col_block, label_prior, seed_label, seed_mask):
    blocks_dev = adjacency_tiles.shape[0]
    degree = adjacency_tiles.shape[1]
    block_rows = adjacency_tiles.shape[2]
    classes = label_prior.shape[1]
    n_rows = lax.axis_size("rows")
    n_cols = lax.axis_size("cols")
    group_size = n_cols * blocks_dev
    own_group = lax.axis_index("rows")
    owner_group = col_block // group_size
    within = col_block % group_size
    table_index = jnp.where(owner_group == own_group, within, group_size + owner_group).reshape(-1)
    anchor = prepare(label_prior, seed_label, seed_mask)
    labels = anchor
    for hop_index in range(HOPS):
        asked = ask_blocks(owner_group, within, own_group, n_rows)
        sent_blocks = labels.astype(jnp.bfloat16).reshape(blocks_dev, block_rows, classes)
        group_blocks = lax.all_gather(sent_blocks, "cols", axis=0, tiled=True)
        reply = group_blocks[asked[:, 0]]
        remote = lax.all_to_all(reply, "rows", split_axis=0, concat_axis=0, tiled=True)
        table = jnp.concatenate([group_blocks, remote], axis=0)
        operand = table[table_index].reshape(blocks_dev, degree, block_rows, classes)
        spread = jnp.einsum(
            "bkij,bkjc->bic", adjacency_tiles, operand, preferred_element_type=jnp.float32
        )
        spread = spread.reshape(blocks_dev * block_rows, classes)
        blended = ALPHA * spread + (1.0 - ALPHA) * anchor
        labels = blended * (classes / jnp.sum(blended, axis=1, keepdims=True))
    return labels


def solution(mesh):
    in_specs = (
        P(("rows", "cols"), None, None, None),
        P(("rows", "cols"), None),
        P(("rows", "cols"), None),
        P(("rows", "cols")),
        P(("rows", "cols")),
    )
    out_specs = P(("rows", "cols"), None)
    return jax.shard_map(local, mesh=mesh, in_specs=in_specs, out_specs=out_specs, check_vma=False)
```

profile of v0, /device:TPU:0, one launch (start us, length us, event | category | flops | bytes accessed | tf_op | source)
XLA Modules:
  0.0 247.3 jit_solution(12359041004204754055)
XLA Ops:
  11.6 13.6 %all_to_all.32 = s32[8,1,1]{2,1,0:T(1,128)S(1)} all-to-all(s32[8,1,1]{2,1,0:T(1,128)S(1)} %copy.8), channel_id=1, replica_groups=mesh['rows'=8,'cols'=4] {'rows'}, dimensions={0} | all-to-all | bytes 64 | tf_op jit(solution)/shard_map/all_to_all | solution.py:27
  25.5 8.3 %all-gather.5.cloned.1.call-done = bf16[24,128,256]{2,1,0:T(8,128)(2,1)} async-done(((bf16[6,128,256]{2,1,0:T(8,128)(2,1)}), bf16[24,128,256]{2,1,0:T(8,128)(2,1)}) %all-gather.5.cloned.1.call-update) | async-done | bytes 1572880 | tf_op jit(solution)/shard_map/all_gather | solution.py:49
  33.7 2.8 %gather_fusion = bf16[8,128,256]{2,1,0:T(8,128)(2,1)} fusion(bf16[24,128,256]{2,1,0:T(8,128)(2,1)} %all-gather.5.cloned.1.call-done, s32[1024]{0:T(1024)S(1)} %pad_clamp_fusion.1), kind=kCustom, calls=%fused_computation | custom fusion | bytes 1048608 | tf_op jit(solution)/shard_map/gather | solution.py:50
  36.5 5.5 %all-to-all-start.1 = ((bf16[8,128,256]{2,1,0:T(8,128)(2,1)}), bf16[8,128,256]{2,1,0:T(8,128)(2,1)S(1)}, u32[]{:S(2)}, u32[]{:S(2)}) async-start(bf16[8,128,256]{2,1,0:T(8,128)(2,1)} %gather_fusion), calls=%async_computation.1 | async-start | bytes 1048576 | tf_op jit(solution)/shard_map/all_to_all | solution.py:51
  42.2 14.7 %all-to-all-done.1 = bf16[8,128,256]{2,1,0:T(8,128)(2,1)S(1)} async-done(((bf16[8,128,256]{2,1,0:T(8,128)(2,1)}), bf16[8,128,256]{2,1,0:T(8,128)(2,1)S(1)}, u32[]{:S(2)}, u32[]{:S(2)}) %all-to-all-start.1) | async-done | bytes 524320 | tf_op jit(solution)/shard_map/all_to_all | solution.py:51
  56.9 3.0 %pad_maximum_fusion = bf16[32,128,256]{2,1,0:T(8,128)(2,1)} fusion(bf16[8,128,256]{2,1,0:T(8,128)(2,1)S(1)} %all-to-all-done.1, bf16[24,128,256]{2,1,0:T(8,128)(2,1)} %all-gather.5.cloned.1.call-done), kind=kLoop, calls=%fused_computation.8 | loop fusion | flops 1048576 | bytes 4194304 | tf_op jit(solution)/shard_map/concatenate | solution.py:52
  59.9 7.1 %gather_fusion.1 = bf16[72,128,256]{2,1,0:T(8,128)(2,1)} fusion(bf16[32,128,256]{2,1,0:T(8,128)(2,1)} %pad_maximum_fusion, s32[1024]{0:T(1024)S(1)} %pad_clamp_fusion), kind=kCustom, calls=%fused_computation.1 | custom fusion | bytes 9437472 | tf_op jit(solution)/shard_map/gather | solution.py:53
  66.9 3.3 %fusion = f32[6,256,128]{1,2,0:T(8,128)S(1)} fusion(bf16[6,12,128,128]{3,2,1,0:T(8,128)(2,1)S(1)} %copy-done, bf16[6,12,128,256]{3,2,1,0:T(8,128)(2,1)} %bitcast.77), kind=kOutput, calls=%fused_computation.16 | convolution fusion | flops 604176384 | bytes 7864320 | tf_op jit(solution)/shard_map/bkij,bkjc->bic/dot_general | solution.py:54
  72.2 17.9 %all-gather.7.cloned.1.call-done = bf16[24,128,256]{2,1,0:T(8,128)(2,1)} async-done(((bf16[6,128,256]{2,1,0:T(8,128)(2,1)}), bf16[24,128,256]{2,1,0:T(8,128)(2,1)}) %all-gather.7.cloned.1.call-update) | async-done | bytes 1572880 | tf_op jit(solution)/shard_map/all_gather | solution.py:49
  90.0 2.8 %gather_fusion.2 = bf16[8,128,256]{2,1,0:T(8,128)(2,1)} fusion(bf16[24,128,256]{2,1,0:T(8,128)(2,1)} %all-gather.7.cloned.1.call-done, s32[1024]{0:T(1024)S(1)} %pad_clamp_fusion.1), kind=kCustom, calls=%fused_computation.2 | custom fusion | bytes 1048608 | tf_op jit(solution)/shard_map/gather | solution.py:50
  92.8 20.4 %all_to_all.33 = bf16[8,128,256]{2,1,0:T(8,128)(2,1)S(1)} all-to-all(bf16[8,128,256]{2,1,0:T(8,128)(2,1)} %gather_fusion.2), channel_id=1, replica_groups=mesh['rows'=8,'cols'=4] {'rows'}, dimensions={0} | all-to-all | bytes 1048576 | tf_op jit(solution)/shard_map/all_to_all | solution.py:51
  113.2 3.0 %pad_maximum_fusion.1 = bf16[32,128,256]{2,1,0:T(8,128)(2,1)} fusion(bf16[8,128,256]{2,1,0:T(8,128)(2,1)S(1)} %all_to_all.33, bf16[24,128,256]{2,1,0:T(8,128)(2,1)} %all-gather.7.cloned.1.call-done), kind=kLoop, calls=%fused_computation.9 | loop fusion | flops 1048576 | bytes 4194304 | tf_op jit(solution)/shard_map/concatenate | solution.py:52
  116.1 7.1 %gather_fusion.3 = bf16[72,128,256]{2,1,0:T(8,128)(2,1)} fusion(bf16[32,128,256]{2,1,0:T(8,128)(2,1)} %pad_maximum_fusion.1, s32[1024]{0:T(1024)S(1)} %pad_clamp_fusion), kind=kCustom, calls=%fused_computation.3 | custom fusion | bytes 9437472 | tf_op jit(solution)/shard_map/gather | solution.py:53
  123.2 3.2 %fusion.1 = f32[6,256,128]{1,2,0:T(8,128)S(1)} fusion(bf16[6,12,128,128]{3,2,1,0:T(8,128)(2,1)S(1)} %copy-done, bf16[6,12,128,256]{3,2,1,0:T(8,128)(2,1)} %bitcast.78), kind=kOutput, calls=%fused_computation.17 | convolution fusion | flops 604176384 | bytes 7864320 | tf_op jit(solution)/shard_map/bkij,bkjc->bic/dot_general | solution.py:54
  128.3 17.9 %all-gather.9.cloned.1.call-done = bf16[24,128,256]{2,1,0:T(8,128)(2,1)} async-done(((bf16[6,128,256]{2,1,0:T(8,128)(2,1)}), bf16[24,128,256]{2,1,0:T(8,128)(2,1)}) %all-gather.9.cloned.1.call-update) | async-done | bytes 1572880 | tf_op jit(solution)/shard_map/all_gather | solution.py:49
  149.0 20.4 %all_to_all.34 = bf16[8,128,256]{2,1,0:T(8,128)(2,1)S(1)} all-to-all(bf16[8,128,256]{2,1,0:T(8,128)(2,1)} %gather_fusion.4), channel_id=1, replica_groups=mesh['rows'=8,'cols'=4] {'rows'}, dimensions={0} | all-to-all | bytes 1048576 | tf_op jit(solution)/shard_map/all_to_all | solution.py:51
  169.4 3.0 %pad_maximum_fusion.2 = bf16[32,128,256]{2,1,0:T(8,128)(2,1)} fusion(bf16[8,128,256]{2,1,0:T(8,128)(2,1)S(1)} %all_to_all.34, bf16[24,128,256]{2,1,0:T(8,128)(2,1)} %all-gather.9.cloned.1.call-done), kind=kLoop, calls=%fused_computation.10 | loop fusion | flops 1048576 | bytes 4194304 | tf_op jit(solution)/shard_map/concatenate | solution.py:52
  172.3 7.1 %gather_fusion.5 = bf16[72,128,256]{2,1,0:T(8,128)(2,1)} fusion(bf16[32,128,256]{2,1,0:T(8,128)(2,1)} %pad_maximum_fusion.2, s32[1024]{0:T(1024)S(1)} %pad_clamp_fusion), kind=kCustom, calls=%fused_computation.5 | custom fusion | bytes 9437472 | tf_op jit(solution)/shard_map/gather | solution.py:53
  179.4 3.2 %fusion.2 = f32[6,256,128]{1,2,0:T(8,128)S(1)} fusion(bf16[6,12,128,128]{3,2,1,0:T(8,128)(2,1)S(1)} %copy-done, bf16[6,12,128,256]{3,2,1,0:T(8,128)(2,1)} %bitcast.79), kind=kOutput, calls=%fused_computation.18 | convolution fusion | flops 604176384 | bytes 7864320 | tf_op jit(solution)/shard_map/bkij,bkjc->bic/dot_general | solution.py:54
  184.5 17.9 %all-gather.11.cloned.1.call-done = bf16[24,128,256]{2,1,0:T(8,128)(2,1)} async-done(((bf16[6,128,256]{2,1,0:T(8,128)(2,1)}), bf16[24,128,256]{2,1,0:T(8,128)(2,1)}) %all-gather.11.cloned.1.call-update) | async-done | bytes 1572880 | tf_op jit(solution)/shard_map/all_gather | solution.py:49
  205.2 20.4 %all_to_all.35 = bf16[8,128,256]{2,1,0:T(8,128)(2,1)S(1)} all-to-all(bf16[8,128,256]{2,1,0:T(8,128)(2,1)} %gather_fusion.6), channel_id=1, replica_groups=mesh['rows'=8,'cols'=4] {'rows'}, dimensions={0} | all-to-all | bytes 1048576 | tf_op jit(solution)/shard_map/all_to_all | solution.py:51
  225.6 3.0 %pad_maximum_fusion.3 = bf16[32,128,256]{2,1,0:T(8,128)(2,1)} fusion(bf16[8,128,256]{2,1,0:T(8,128)(2,1)S(1)} %all_to_all.35, bf16[24,128,256]{2,1,0:T(8,128)(2,1)} %all-gather.11.cloned.1.call-done), kind=kLoop, calls=%fused_computation.11 | loop fusion | flops 1048576 | bytes 4194304 | tf_op jit(solution)/shard_map/concatenate | solution.py:52
  228.5 7.1 %gather_fusion.7 = bf16[72,128,256]{2,1,0:T(8,128)(2,1)} fusion(bf16[32,128,256]{2,1,0:T(8,128)(2,1)} %pad_maximum_fusion.3, s32[1024]{0:T(1024)S(1)} %pad_clamp_fusion), kind=kCustom, calls=%fused_computation.7 | custom fusion | bytes 9437472 | tf_op jit(solution)/shard_map/gather | solution.py:53
  235.6 3.2 %fusion.3 = f32[6,256,128]{1,2,0:T(8,128)S(1)} fusion(bf16[6,12,128,128]{3,2,1,0:T(8,128)(2,1)S(1)} %copy-done, bf16[6,12,128,256]{3,2,1,0:T(8,128)(2,1)} %bitcast.76), kind=kOutput, calls=%fused_computation.19 | convolution fusion | flops 604176384 | bytes 7864320 | tf_op jit(solution)/shard_map/bkij,bkjc->bic/dot_general | solution.py:54
  (46 shorter events, 18.4 us)
Async XLA Ops:
  6.5 60.4 %copy-start = (bf16[6,12,128,128]{3,2,1,0:T(8,128)(2,1)S(1)}, bf16[6,12,128,128]{3,2,1,0:T(8,128)(2,1)}, u32[]{:S(2)}) copy-start(bf16[6,12,128,128]{3,2,1,0:T(8,128)(2,1)} %param.5) | copy-start | bytes 7077892
  6.5 4.7 %copy-start.3 = (s32[6,12]{1,0:T(8,128)S(1)}, s32[6,12]{1,0:T(8,128)}, u32[]{:S(2)}) copy-start(s32[6,12]{1,0:T(8,128)} %param.6) | copy-start | bytes 868
  6.5 27.2 %all-gather.5.cloned.1.call-start = ((), (), s32[]{:S(2)}) async-start(), calls=%async_computation.5 | async-start | bytes 1966080 | tf_op jit(solution)/shard_map/all_gather | solution.py:49
  36.5 20.4 %all-to-all-start.1 = ((bf16[8,128,256]{2,1,0:T(8,128)(2,1)}), bf16[8,128,256]{2,1,0:T(8,128)(2,1)S(1)}, u32[]{:S(2)}, u32[]{:S(2)}) async-start(bf16[8,128,256]{2,1,0:T(8,128)(2,1)} %gather_fusion), calls=%async_computation.1 | async-start | bytes 1048576 | tf_op jit(solution)/shard_map/all_to_all | solution.py:51
  42.0 48.0 %all-gather.7.cloned.1.call-start = ((), (), s32[]{:S(2)}) async-start(), calls=%async_computation.6 | async-start | bytes 1966080 | tf_op jit(solution)/shard_map/all_gather | solution.py:49
  66.9 3.3 %copy-start.1 = (f32[768,256]{1,0:T(8,128)S(1)}, f32[768,256]{1,0:T(8,128)}, u32[]{:S(2)}) copy-start(f32[768,256]{1,0:T(8,128)} %param.7) | copy-start | bytes 2359300
  66.9 3.3 %copy-start.2 = (s32[768]{0:T(1024)S(1)}, s32[768]{0:T(1024)}, u32[]{:S(2)}) copy-start(s32[768]{0:T(1024)} %param.8) | copy-start | bytes 9220
  72.1 74.1 %all-gather.9.cloned.1.call-start = ((), (), s32[]{:S(2)}) async-start(), calls=%async_computation.7 | async-start | bytes 1966080 | tf_op jit(solution)/shard_map/all_gather | solution.py:49
  128.3 74.1 %all-gather.11.cloned.1.call-start = ((), (), s32[]{:S(2)}) async-start(), calls=%async_computation.8 | async-start | bytes 1966080 | tf_op jit(solution)/shard_map/all_gather | solution.py:49
Sparse Core Ops, SparseCore 0:
  11.3 22.3 all-gather.4
  72.2 17.7 all-gather.6
  128.4 17.7 all-gather.8
  184.6 17.7 all-gather.10
where the time goes:
time: 248 us; the launch traced here: 247 us
  waiting for transfers between devices  76.7 us (31%)
  blocking collectives  74.8 us (30%)
  local copies, waits for them, and re-layouts  39.7 us (16%)
  other arithmetic  24.2 us (10%)
  between operations  13.3 us (5%)
  matrix products  13 us (5%)
  starting transfers between devices  5.64 us (2%)
    all_gather x4, waiting for transfers between devices, local(): group_blocks = lax.all_gather(sent_blocks, 'cols', axis=0, tiled=True)  61.9 us
    all_to_all x3, blocking collectives, local(): lax.all_to_all(reply, 'rows', split_axis=0, concat_axis=0, tiled=True)  61.2 us
    gather x4, local copies, waits for them, and re-layouts, local(): table[table_index].reshape(blocks_dev, degree, block_rows, classes)  28.3 us
    all_to_all x1, waiting for transfers between devices, local(): lax.all_to_all(reply, 'rows', split_axis=0, concat_axis=0, tiled=True)  14.7 us
    all_to_all x1, blocking collectives, ask_blocks(): lax.all_to_all(wanted.reshape(n_rows, 1), 'rows', split_axis=0, concat_ax...  13.6 us
    dot_general x4, matrix products, local(): jnp.einsum('bkij,bkjc->bic', adjacency_tiles, operand, preferred_element_...  13 us
    concatenate x4, other arithmetic, local(): table = jnp.concatenate([group_blocks, remote], axis=0)  11.8 us
    gather x4, local copies, waits for them, and re-layouts, local(): reply = group_blocks[asked[:, 0]]  11.1 us
  transfers between devices with their start and end apart: 5, of which 5 were waited for; matrix products, arithmetic and copies ran while one was open for 0% of the time, Pallas kernels for 0%

commit v1 on v0

v1 whole, which is shorter than its diff:
```python
import functools

import jax
import jax.numpy as jnp
from jax import lax
from jax.experimental import pallas as pl
from jax.experimental.pallas import tpu as pltpu
from jax.sharding import PartitionSpec as P

HOPS = 4
CHUNKS = 4
ALPHA = 0.85
SEED_BOOST = 8.0
LANES = 128
MESH = pl.DeviceIdType.MESH


def prepare(label_prior, seed_label, seed_mask):
    classes = label_prior.shape[1]
    one_hot = (seed_label[:, None] == jnp.arange(classes, dtype=jnp.int32)[None, :]).astype(
        jnp.float32
    )
    anchor_raw = label_prior + SEED_BOOST * seed_mask[:, None].astype(jnp.float32) * one_hot
    return anchor_raw * (classes / jnp.sum(anchor_raw, axis=1, keepdims=True))


def kernel(
    n_rows, n_cols, blocks_dev, degree, block_rows, classes,
    index_ref, wanted_ref, anchor_ref, adj_hbm, out_ref,
    tables, remote, reply, adj, asked_v, asked_s,
    adj_sem, asked_send, asked_recv, asked_copy,
    near_send, near_recv, far_send, far_recv, fwd_send, fwd_recv, rep_send, rep_recv,
):
    row = lax.axis_index("rows")
    col = lax.axis_index("cols")
    group = n_cols * blocks_dev
    width = 2 if n_cols % 2 == 0 else 1
    pairs = n_cols // width
    pair, low = col // width, col % width
    mate = pair * width + (width - 1 - low)
    chunk = block_rows // CHUNKS
    peers = n_rows - 1

    def far_col(j):
        return ((pair + j) % pairs) * width + low

    def from_col(j):
        return ((pair + pairs - j) % pairs) * width + low

    def each_peer(body):
        half = n_rows // 2
        def step(i):
            if isinstance(i, int):
                d = half + ((i + 1) // 2) * (1 - 2 * (i % 2))
            else:
                d = half + lax.div(i + 1, 2) * (1 - 2 * lax.rem(i, 2))
            body((row + d + n_rows) % n_rows)
        if n_rows <= 8:
            for i in range(peers):
                step(i)
        else:
            def loop(i, carry):
                step(i)
                return carry
            lax.fori_loop(0, peers, loop, 0)

    adj_copy = pltpu.make_async_copy(adj_hbm, adj, adj_sem)
    adj_copy.start()

    barrier = pltpu.get_barrier_semaphore()
    greeted = peers
    if width == 2:
        pl.semaphore_signal(barrier, inc=1, device_id=(row, mate), device_id_type=MESH)
        greeted += 1
    for j in range(1, pairs):
        pl.semaphore_signal(barrier, inc=1, device_id=(row, far_col(j)), device_id_type=MESH)
        greeted += 1
    each_peer(
        lambda other: pl.semaphore_signal(
            barrier, inc=1, device_id=(other, col), device_id_type=MESH
        )
    )
    def keep(p, b, labels):
        sent = labels.astype(jnp.bfloat16)
        for q in range(CHUNKS):
            tables[p][q][col * blocks_dev + b] = sent[q * chunk : (q + 1) * chunk, :]

    for b in range(blocks_dev):
        keep(0, b, anchor_ref[b * block_rows : (b + 1) * block_rows, :])
    pl.semaphore_wait(barrier, greeted)

    def part(p, owner, q):
        return tables[p][q].at[pl.ds(owner * blocks_dev, blocks_dev)]

    def near(p, q):
        ref = part(p, col, q)
        return pltpu.make_async_remote_copy(
            src_ref=ref, dst_ref=ref, send_sem=near_send.at[p, q], recv_sem=near_recv.at[p, q],
            device_id=(row, mate), device_id_type=MESH,
        )

    def far(p, j, q):
        ref = part(p, col, q)
        return pltpu.make_async_remote_copy(
            src_ref=ref, dst_ref=ref,
            send_sem=far_send.at[p, j - 1, q], recv_sem=far_recv.at[p, j - 1, q],
            device_id=(row, far_col(j)), device_id_type=MESH,
        )

    def forward(p, j, q):
        ref = part(p, from_col(j), q)
        return pltpu.make_async_remote_copy(
            src_ref=ref, dst_ref=ref,
            send_sem=fwd_send.at[p, j - 1, q], recv_sem=fwd_recv.at[p, j - 1, q],
            device_id=(row, mate), device_id_type=MESH,
        )

    def start_gather(p):
        for q in range(CHUNKS):
            for j in range(1, pairs):
                far(p, j, q).start()
            if width == 2:
                near(p, q).start()

    start_gather(0)

    def send_wanted(other):
        pltpu.make_async_remote_copy(
            src_ref=wanted_ref, dst_ref=asked_v.at[row], send_sem=asked_send, recv_sem=asked_recv,
            device_id=(other, col), device_id_type=MESH,
        ).start()

    each_peer(send_wanted)
    all_asked = asked_v.at[pl.ds(0, peers)]
    pltpu.make_async_copy(all_asked, all_asked, asked_recv).wait()
    pltpu.make_async_copy(all_asked, all_asked, asked_send).wait()
    to_scalar = pltpu.make_async_copy(asked_v, asked_s, asked_copy)
    to_scalar.start()
    to_scalar.wait()
    adj_copy.wait()

    def load(p, b, k):
        index = index_ref[b * degree + k]
        return [tables[p][q][index] for q in range(CHUNKS)]

    def hop(p, last):
        for q in range(CHUNKS):
            rows_q = pl.ds(q * chunk, chunk)
            for j in range(1, pairs):
                far(p, j, q).wait_recv()
                if width == 2:
                    forward(p, j, q).start()
            if width == 2:
                near(p, q).wait_recv()
                for j in range(1, pairs):
                    forward(p, j, q).wait_recv()

            def answer(other):
                reply[other, rows_q, :] = tables[p][q][asked_s[other, 0, row]]
                pltpu.make_async_remote_copy(
                    src_ref=reply.at[other, rows_q, :],
                    dst_ref=remote.at[p, row, rows_q, :],
                    send_sem=rep_send.at[p], recv_sem=rep_recv.at[p],
                    device_id=(other, col), device_id_type=MESH,
                ).start()

            each_peer(answer)
        got = remote.at[p, pl.ds(0, peers)]
        pltpu.make_async_copy(got, got, rep_recv.at[p]).wait()

        def fold(other):
            for q in range(CHUNKS):
                tables[p][q][group + other] = remote[p, other, pl.ds(q * chunk, chunk), :]

        each_peer(fold)

        step = 2 if degree % 2 == 0 else 1
        for b in range(blocks_dev):
            spread = jnp.zeros((block_rows, classes), jnp.float32)
            for k in range(0, degree, step):
                lhs = jnp.concatenate([adj[b, k + i] for i in range(step)], axis=1)
                rhs = jnp.concatenate(sum([load(p, b, k + i) for i in range(step)], []), axis=0)
                spread = spread + jnp.dot(lhs, rhs, preferred_element_type=jnp.float32)
            here = slice(b * block_rows, (b + 1) * block_rows)
            blended = ALPHA * spread + (1.0 - ALPHA) * anchor_ref[here, :]
            labels = blended * (classes / jnp.sum(blended, axis=1, keepdims=True))
            out_ref[here, :] = labels
            keep(1 - p, b, labels)

        for q in range(CHUNKS):
            for j in range(1, pairs):
                far(p, j, q).wait_send()
                if width == 2:
                    forward(p, j, q).wait_send()
            if width == 2:
                near(p, q).wait_send()
        sent = reply.at[pl.ds(0, peers)]
        pltpu.make_async_copy(sent, sent, rep_send.at[p]).wait()

        if not last:
            start_gather(1 - p)

    for h in range(HOPS):
        hop(h % 2, h == HOPS - 1)


def local(adjacency_tiles, col_block, label_prior, seed_label, seed_mask):
    blocks_dev, degree, block_rows, _ = adjacency_tiles.shape
    nodes, classes = label_prior.shape
    n_rows = lax.axis_size("rows")
    n_cols = lax.axis_size("cols")
    group = n_cols * blocks_dev
    own_group = lax.axis_index("rows")
    owner_group = col_block // group
    within = col_block % group
    table_index = jnp.where(owner_group == own_group, within, group + owner_group).reshape(-1)
    padded = -(-n_rows // LANES) * LANES
    group_ids = jnp.arange(padded, dtype=jnp.int32)
    matched = owner_group.reshape(-1)[:, None] == group_ids[None, :]
    wanted = jnp.max(jnp.where(matched, within.reshape(-1)[:, None], 0), axis=0)[None, :]
    anchor = prepare(label_prior, seed_label, seed_mask)
    pairs = max(n_cols // 2 if n_cols % 2 == 0 else n_cols, 2)
    dma = pltpu.SemaphoreType.DMA
    vmem = pl.BlockSpec(memory_space=pltpu.VMEM)
    return pl.pallas_call(
        functools.partial(kernel, n_rows, n_cols, blocks_dev, degree, block_rows, classes),
        out_shape=jax.ShapeDtypeStruct((nodes, classes), jnp.float32),
        in_specs=[
            pl.BlockSpec(memory_space=pltpu.SMEM),
            vmem,
            vmem,
            pl.BlockSpec(memory_space=pl.ANY),
        ],
        out_specs=vmem,
        scratch_shapes=[
            [
                [
                    pltpu.VMEM((group + n_rows, block_rows // CHUNKS, classes), jnp.bfloat16)
                    for _ in range(CHUNKS)
                ]
                for _ in range(2)
            ],
            pltpu.VMEM((2, n_rows, block_rows, classes), jnp.bfloat16),
            pltpu.VMEM((n_rows, block_rows, classes), jnp.bfloat16),
            pltpu.VMEM(adjacency_tiles.shape, jnp.bfloat16),
            pltpu.VMEM((n_rows, 1, padded), jnp.int32),
            pltpu.SMEM((n_rows, 1, padded), jnp.int32),
            dma, dma, dma, dma,
            dma((2, CHUNKS)), dma((2, CHUNKS)),
            dma((2, pairs - 1, CHUNKS)), dma((2, pairs - 1, CHUNKS)),
            dma((2, pairs - 1, CHUNKS)), dma((2, pairs - 1, CHUNKS)),
            dma((2,)), dma((2,)),
        ],
        compiler_params=pltpu.CompilerParams(
            collective_id=0, has_side_effects=True, vmem_limit_bytes=60 * 1024 * 1024
        ),
    )(table_index, wanted, anchor, adjacency_tiles)


def solution(mesh):
    in_specs = (
        P(("rows", "cols"), None, None, None),
        P(("rows", "cols"), None),
        P(("rows", "cols"), None),
        P(("rows", "cols")),
        P(("rows", "cols")),
    )
    out_specs = P(("rows", "cols"), None)
    return jax.shard_map(local, mesh=mesh, in_specs=in_specs, out_specs=out_specs, check_vma=False)
```

time: 248 us -> 94.7 us (0.38)
  Pallas kernels: 0 us -> 85.6 us
  waiting for transfers between devices: 76.7 us -> 0 us
  blocking collectives: 74.8 us -> 0 us
  local copies, waits for them, and re-layouts: 39.7 us -> 2.87 us
  other arithmetic: 24.2 us -> 5.9 us
  between operations: 13.3 us -> 0.02 us
  matrix products: 13 us -> 0 us
  starting transfers between devices: 5.64 us -> 0 us
    pallas_call x0 -> x1, Pallas kernels: none -> 85.6 us  [local(): pl.pallas_call(functools.partial(kernel, n_rows, n_cols, blocks_dev, degr...]
    all_to_all x4 -> x0, blocking collectives: 74.8 us -> none  [the longest x3 61.2 us: local(): lax.all_to_all(reply, 'rows', split_axis=0, concat_axis=0, tiled=True)]
    all_gather x4 -> x0, waiting for transfers between devices: 61.9 us -> none  [local(): group_blocks = lax.all_gather(sent_blocks, 'cols', axis=0, tiled=True)]
    gather x8 -> x0, local copies, waits for them, and re-layouts: 39.4 us -> none  [the longest x4 28.3 us: local(): table[table_index].reshape(blocks_dev, degree, block_rows, classes)]
    all_to_all x1 -> x0, waiting for transfers between devices: 14.7 us -> none  [local(): lax.all_to_all(reply, 'rows', split_axis=0, concat_axis=0, tiled=True)]
    dot_general x4 -> x0, matrix products: 13 us -> none  [local(): jnp.einsum('bkij,bkjc->bic', adjacency_tiles, operand, preferred_element_...]
    concatenate x4 -> x0, other arithmetic: 11.8 us -> none  [local(): table = jnp.concatenate([group_blocks, remote], axis=0)]
    convert_element_type x4 -> x0, other arithmetic: 6.04 us -> none  [local(): labels.astype(jnp.bfloat16).reshape(blocks_dev, block_rows, classes)]
  transfers between devices with their start and end apart: 5 -> 0, of which waited for: 5 -> 0; matrix products, arithmetic and copies ran while one was open for 0% -> 0% of each run, Pallas kernels for 0% -> 0%
where the time goes in v1:
time: 94.7 us; the launch traced here: 94.4 us
  Pallas kernels  85.6 us (90%)
  other arithmetic  5.9 us (6%)
  local copies, waits for them, and re-layouts  2.87 us (3%)
    pallas_call x1, Pallas kernels, local(): pl.pallas_call(functools.partial(kernel, n_rows, n_cols, blocks_dev, degr...  85.6 us
    mul x1, other arithmetic, prepare(): return anchor_raw * (classes / jnp.sum(anchor_raw, axis=1, keepdims=True))  2.38 us
    unnamed x1, local copies, waits for them, and re-layouts  2.06 us

profile of v1, /device:TPU:0, one launch (start us, length us, event | category | flops | bytes accessed | tf_op | source)
XLA Modules:
  0.0 94.4 jit_solution(3675925535395046794)
XLA Ops:
  0.0 0.7 convert_multiply_fusion
  0.7 1.5 %fusion.1 = f32[768]{0:T(1024)S(1)} fusion(f32[768,256]{1,0:T(8,128)} %param.7, f32[768]{0:T(1024)S(1)} %convert_multiply_fusion, s32[768]{0:T(1024)} %param.8), kind=kLoop, calls=%fused_computation.3 | loop fusion | flops 785664 | bytes 795648 | tf_op jit(solution)/shard_map/reduce_sum | solution.py:24
  2.2 0.7 add_select_fusion.1
  2.9 0.1 eq.38
  3.0 0.7 reshape.13.index_ref
  3.7 0.1 broadcast_in_dim.22
  3.8 0.6 select_reduce_fusion
  4.3 2.4 %fusion.anchor_ref = f32[768,256]{1,0:T(8,128)} fusion(f32[768,256]{1,0:T(8,128)} %param.7, f32[768]{0:T(1024)S(1)} %broadcast_divide_fusion, f32[768]{0:T(1024)S(1)} %convert_multiply_fusion, s32[768]{0:T(1024)} %param.8), kind=kLoop, calls=%fused_computation.2 | loop fusion | flops 786432 | bytes 1582080 | tf_op jit(solution)/shard_map/mul | solution.py:24
  6.7 85.6 %shard_map.55 = f32[768,256]{1,0:T(8,128)} custom-call(s32[72]{0:T(128)} %reshape.13.index_ref, s32[1,128]{1,0:T(1,128)} %bitcast.1, f32[768,256]{1,0:T(8,128)} %fusion.anchor_ref, bf16[6,12,128,128]{3,2,1,0:T(8,128)(2,1)} %adj_hbm.1), custom_call_target="tpu_custom_call" | custom-call | tf_op jit(solution)/shard_map/pallas_call | solution.py:225
  92.3 2.1 %copy.7 = f32[768,256]{1,0:T(8,128)} copy(f32[768,256]{1,0:T(8,128)} %shard_map.55) | data formatting | bytes 1572864
  (1 shorter events, 0.0 us)

commit v2 on v1

--- a/solution.py
+++ b/solution.py
@@ -8,26 +8,18 @@
 from jax.sharding import PartitionSpec as P
 
 HOPS = 4
-CHUNKS = 4
+CHUNK_PARTS = (1, 1, 2, 2, 2)
+CHUNKS = len(CHUNK_PARTS)
 ALPHA = 0.85
 SEED_BOOST = 8.0
 LANES = 128
 MESH = pl.DeviceIdType.MESH
 
 
-def prepare(label_prior, seed_label, seed_mask):
-    classes = label_prior.shape[1]
-    one_hot = (seed_label[:, None] == jnp.arange(classes, dtype=jnp.int32)[None, :]).astype(
-        jnp.float32
-    )
-    anchor_raw = label_prior + SEED_BOOST * seed_mask[:, None].astype(jnp.float32) * one_hot
-    return anchor_raw * (classes / jnp.sum(anchor_raw, axis=1, keepdims=True))
-
-
 def kernel(
     n_rows, n_cols, blocks_dev, degree, block_rows, classes,
-    index_ref, wanted_ref, anchor_ref, adj_hbm, out_ref,
-    tables, remote, reply, adj, asked_v, asked_s,
+    col_block_ref, prior_ref, label_ref, mask_ref, adj_hbm, out_ref,
+    tables, remote, reply, adj, anchor_ref, index_ref, wanted_ref, asked_v, asked_s,
     adj_sem, asked_send, asked_recv, asked_copy,
     near_send, near_recv, far_send, far_recv, fwd_send, fwd_recv, rep_send, rep_recv,
 ):
@@ -38,7 +30,9 @@
     pairs = n_cols // width
     pair, low = col // width, col % width
     mate = pair * width + (width - 1 - low)
-    chunk = block_rows // CHUNKS
+    unit = block_rows // sum(CHUNK_PARTS)
+    starts = [unit * sum(CHUNK_PARTS[:q]) for q in range(CHUNKS)]
+    sizes = [unit * part for part in CHUNK_PARTS]
     peers = n_rows - 1
 
     def far_col(j):
@@ -83,10 +77,18 @@
     def keep(p, b, labels):
         sent = labels.astype(jnp.bfloat16)
         for q in range(CHUNKS):
-            tables[p][q][col * blocks_dev + b] = sent[q * chunk : (q + 1) * chunk, :]
-
+            tables[p][q][col * blocks_dev + b] = sent[starts[q] : starts[q] + sizes[q], :]
+
+    code = jnp.where(mask_ref[...] > 0, label_ref[...], -1)
     for b in range(blocks_dev):
-        keep(0, b, anchor_ref[b * block_rows : (b + 1) * block_rows, :])
+        here = slice(b * block_rows, (b + 1) * block_rows)
+        across = jnp.broadcast_to(code[b : b + 1, :], (block_rows, block_rows)).T
+        class_id = lax.broadcasted_iota(jnp.int32, (block_rows, classes), 1)
+        across = jnp.concatenate([across] * (classes // block_rows), axis=1)
+        raw = prior_ref[here, :] + jnp.where(class_id == across, SEED_BOOST, 0.0)
+        anchor = raw * (classes / jnp.sum(raw, axis=1, keepdims=True))
+        anchor_ref[here, :] = anchor
+        keep(0, b, anchor)
     pl.semaphore_wait(barrier, greeted)
 
     def part(p, owner, q):
@@ -123,6 +125,17 @@
                 near(p, q).start()
 
     start_gather(0)
+
+    lane = lax.broadcasted_iota(jnp.int32, wanted_ref.shape, 1)
+    wanted = jnp.zeros(wanted_ref.shape, jnp.int32)
+    for b in range(blocks_dev):
+        for k in range(degree):
+            block = col_block_ref[b, k]
+            owner = lax.div(block, group)
+            within = block - owner * group
+            index_ref[b * degree + k] = jnp.where(owner == row, within, group + owner)
+            wanted = jnp.where(lane == owner, within, wanted)
+    wanted_ref[...] = wanted
 
     def send_wanted(other):
         pltpu.make_async_remote_copy(
@@ -145,7 +158,7 @@
 
     def hop(p, last):
         for q in range(CHUNKS):
-            rows_q = pl.ds(q * chunk, chunk)
+            rows_q = pl.ds(starts[q], sizes[q])
             for j in range(1, pairs):
                 far(p, j, q).wait_recv()
                 if width == 2:
@@ -170,7 +183,7 @@
 
         def fold(other):
             for q in range(CHUNKS):
-                tables[p][q][group + other] = remote[p, other, pl.ds(q * chunk, chunk), :]
+                tables[p][q][group + other] = remote[p, other, pl.ds(starts[q], sizes[q]), :]
 
         each_peer(fold)
 
@@ -210,16 +223,12 @@
     n_rows = lax.axis_size("rows")
     n_cols = lax.axis_size("cols")
     group = n_cols * blocks_dev
-    own_group = lax.axis_index("rows")
-    owner_group = col_block // group
-    within = col_block % group
-    table_index = jnp.where(owner_group == own_group, within, group + owner_group).reshape(-1)
     padded = -(-n_rows // LANES) * LANES
-    group_ids = jnp.arange(padded, dtype=jnp.int32)
-    matched = owner_group.reshape(-1)[:, None] == group_ids[None, :]
-    wanted = jnp.max(jnp.where(matched, within.reshape(-1)[:, None], 0), axis=0)[None, :]
-    anchor = prepare(label_prior, seed_label, seed_mask)
     pairs = max(n_cols // 2 if n_cols % 2 == 0 else n_cols, 2)
+    unit = block_rows // sum(CHUNK_PARTS)
+    block_bytes = 2 * block_rows * classes
+    held = (2 * (group + n_rows) + 3 * n_rows) * block_bytes
+    held += 2 * adjacency_tiles.size + 3 * 4 * nodes * classes
     dma = pltpu.SemaphoreType.DMA
     vmem = pl.BlockSpec(memory_space=pltpu.VMEM)
     return pl.pallas_call(
@@ -229,20 +238,24 @@
             pl.BlockSpec(memory_space=pltpu.SMEM),
             vmem,
             vmem,
-            pl.BlockSpec(memory_space=pl.ANY),
+            vmem,
+            pl.BlockSpec(memory_space=pltpu.HBM),
         ],
         out_specs=vmem,
         scratch_shapes=[
             [
                 [
-                    pltpu.VMEM((group + n_rows, block_rows // CHUNKS, classes), jnp.bfloat16)
-                    for _ in range(CHUNKS)
+                    pltpu.VMEM((group + n_rows, unit * part, classes), jnp.bfloat16)
+                    for part in CHUNK_PARTS
                 ]
                 for _ in range(2)
             ],
             pltpu.VMEM((2, n_rows, block_rows, classes), jnp.bfloat16),
             pltpu.VMEM((n_rows, block_rows, classes), jnp.bfloat16),
             pltpu.VMEM(adjacency_tiles.shape, jnp.bfloat16),
+            pltpu.VMEM((nodes, classes), jnp.float32),
+            pltpu.SMEM((blocks_dev * degree,), jnp.int32),
+            pltpu.VMEM((1, padded), jnp.int32),
             pltpu.VMEM((n_rows, 1, padded), jnp.int32),
             pltpu.SMEM((n_rows, 1, padded), jnp.int32),
             dma, dma, dma, dma,
@@ -252,9 +265,15 @@
             dma((2,)), dma((2,)),
         ],
         compiler_params=pltpu.CompilerParams(
-            collective_id=0, has_side_effects=True, vmem_limit_bytes=60 * 1024 * 1024
+            collective_id=0, has_side_effects=True, vmem_limit_bytes=held + 6 * 1024 * 1024
         ),
-    )(table_index, wanted, anchor, adjacency_tiles)
+    )(
+        col_block,
+        label_prior,
+        seed_label.reshape(blocks_dev, block_rows),
+        seed_mask.reshape(blocks_dev, block_rows),
+        adjacency_tiles,
+    )
 
 
 def solution(mesh):

time: 94.7 us -> 89.4 us (0.944)
  other arithmetic: 5.9 us -> 0 us
  local copies, waits for them, and re-layouts: 2.87 us -> 5.74 us
  Pallas kernels: 85.6 us -> 83.4 us
    unnamed x1 -> x11, local copies, waits for them, and re-layouts: 2.06 us -> 5.74 us
    mul x2 -> x0, other arithmetic: 3.07 us -> none  [the longest x1 2.38 us: prepare(): return anchor_raw * (classes / jnp.sum(anchor_raw, axis=1, keepdims=True))]
    pallas_call x1, Pallas kernels: 85.6 us -> 83.4 us  [local(): pl.pallas_call(functools.partial(kernel, n_rows, n_cols, blocks_dev, degr...]
    reduce_sum x1 -> x0, other arithmetic: 1.53 us -> none  [prepare(): return anchor_raw * (classes / jnp.sum(anchor_raw, axis=1, keepdims=True))]
where the time goes in v2:
time: 89.4 us; the launch traced here: 89.2 us
  Pallas kernels  83.4 us (93%)
  local copies, waits for them, and re-layouts  5.74 us (6%)
    pallas_call x1, Pallas kernels, local(): pl.pallas_call(functools.partial(kernel, n_rows, n_cols, blocks_dev, degr...  83.4 us
    unnamed x11, local copies, waits for them, and re-layouts  5.74 us

profile of v2, /device:TPU:0, one launch (start us, length us, event | category | flops | bytes accessed | tf_op | source)
XLA Modules:
  0.0 89.2 jit_solution(8162787463927577535)
XLA Ops:
  0.0 0.0 copy-start
  0.0 1.7 %copy-done = bf16[6,12,128,128]{3,2,1,0:T(8,128)(2,1)S(1)} copy-done((bf16[6,12,128,128]{3,2,1,0:T(8,128)(2,1)S(1)}, bf16[6,12,128,128]{3,2,1,0:T(8,128)(2,1)}, u32[]{:S(2)}) %copy-start) | copy-done | bytes 2359320
  1.7 0.0 copy-start.1
  1.7 1.1 %copy-done.1 = f32[768,256]{1,0:T(8,128)S(1)} copy-done((f32[768,256]{1,0:T(8,128)S(1)}, f32[768,256]{1,0:T(8,128)}, u32[]{:S(2)}) %copy-start.1) | copy-done | bytes 786456
  2.8 0.0 copy-start.2
  2.8 0.7 copy-done.2
  3.5 0.0 copy-start.3
  3.5 0.7 copy-done.3
  4.2 0.0 copy-start.4
  4.2 0.7 copy-done.4
  4.9 83.4 %shard_map.55 = f32[768,256]{1,0:T(8,128)S(1)} custom-call(s32[6,12]{1,0:T(8,128)S(1)} %copy-done.2, f32[768,256]{1,0:T(8,128)S(1)} %copy-done.1, s32[6,128]{1,0:T(8,128)S(1)} %bitcast.2, s32[6,128]{1,0:T(8,128)S(1)} %bitcast.3, bf16[6,12,128,128]{3,2,1,0:T(8,128)(2,1)S(1)} %copy-done), custom_call_target="tpu_custom_call" | custom-call | tf_op jit(solution)/shard_map/pallas_call | solution.py:234
  88.3 0.9 copy.7
Async XLA Ops:
  0.0 1.7 %copy-start = (bf16[6,12,128,128]{3,2,1,0:T(8,128)(2,1)S(1)}, bf16[6,12,128,128]{3,2,1,0:T(8,128)(2,1)}, u32[]{:S(2)}) copy-start(bf16[6,12,128,128]{3,2,1,0:T(8,128)(2,1)} %adj_hbm.1) | copy-start | bytes 7077892
  1.7 1.1 %copy-start.1 = (f32[768,256]{1,0:T(8,128)S(1)}, f32[768,256]{1,0:T(8,128)}, u32[]{:S(2)}) copy-start(f32[768,256]{1,0:T(8,128)} %prior_ref.1) | copy-start | bytes 2359300
  2.8 0.7 copy-start.2
  3.5 0.7 copy-start.3
  4.2 0.7 copy-start.4
